TPU v7x, 256 devices: a whole 4x4x8 slice. The times are simulated.
256 devices in a mesh: batch: 8 (over x, y_lo), seq: 16 (over y_hi, z), head: 2 (over core).
Axes of the slice: x: 4, y: 4 (y_hi: 2, y_lo: 2; y = y_hi * 2 + y_lo), z: 8, core: 2. Of those that a mesh axis runs over, the one named last changes fastest.
Arguments:
- queries: bfloat16 [1, 49152, 2048], P(None, ('batch', 'seq'), 'head'), parts along dimension 1, may hold values from -240 to 240
- keys: bfloat16 [1, 49152, 1024], P(None, ('batch', 'seq'), 'head'), parts along dimension 1, may hold values from -6 to 6
- values: bfloat16 [1, 49152, 1024], P(None, ('batch', 'seq'), 'head'), parts along dimension 1, may hold values from -6 to 6
- exit_layer: int32 [384], P(('batch', 'seq')), parts along dimension 0, may hold values from 0 to 1
- tile_order: int32 [384], P('batch'), parts along dimension 0, may hold values from 0 to 47, each once
Outputs:
- attended: bfloat16 [1, 49152, 2048], P(None, ('batch', 'seq'), 'head'), parts along dimension 1
- live_tiles: int32 [8], P('batch'), parts along dimension 0
There are 8 independent parts, one for each index of `batch`. A program takes and returns all parts, laid end to end along the dimension named above; each array names one. Nothing has to cross between parts.
Inputs may be any that keep to these rules, and one draw needn't show every extreme that they name: Tile t covers tokens t * 128 to t * 128 + 127 of the token dimension; tile_order is a permutation of 0 to 47.
All inputs are finite; a program needn't handle non-finite values.
Results may differ from a plain program's by a relative error of at most 0.0049.
Values may be sent and summed in bfloat16 or wider, within the bound.
A program may use at most 128 MiB of HBM per device.

v0:
```python
import math

import jax
import jax.numpy as jnp
from jax import lax
from jax.sharding import Mesh
from jax.sharding import PartitionSpec as P

HD = 256
TILE = 128
SEQ = ("seq_0", "seq_1")
BATCH_SEQ = ("batch", "seq_0", "seq_1")


softcap = 50.0
query_scale = 0.0625


def side_by_side(arrays, axis, dim, along):
    both = jnp.concatenate(arrays, axis=along)
    whole, at, gathered = (lax.all_gather(both, axis, axis=dim, tiled=True), 0, [])
    for a in arrays:
        gathered.append(lax.slice_in_dim(whole, at, at + a.shape[along], axis=along))
        at += a.shape[along]
    return tuple(gathered)


def by_axis(x, axes):
    for axis in axes:
        x = lax.psum(x, axis)
    return x


def lookup(lookup_table, wanted):
    table_slots = jnp.arange(lookup_table.shape[0], dtype=jnp.int32)
    picked = jnp.where(wanted[:, None] == table_slots[None, :], lookup_table[None, :], 0)
    return jnp.sum(picked, axis=1)


def token_positions(tile_order, first_row, row_count):
    offsets = first_row + jnp.arange(row_count, dtype=jnp.int32)
    return lookup(tile_order, offsets // TILE) * TILE + offsets % TILE


def attend(carried, key_rows, value_rows, key_pos, grouped, query_pos):
    row_count = key_rows.shape[0]
    kv_here = grouped.shape[1]
    block_rows = math.gcd(row_count, 512)
    key_heads = key_rows.reshape(row_count, kv_here, HD)
    value_heads = value_rows.reshape(row_count, kv_here, HD)

    def one_block(block_index, running):
        numerator, denominator = running
        lower_row = block_index * block_rows
        key_block = lax.dynamic_slice_in_dim(key_heads, lower_row, block_rows, 0)
        value_block = lax.dynamic_slice_in_dim(value_heads, lower_row, block_rows, 0)
        pos_block = lax.dynamic_slice_in_dim(key_pos, lower_row, block_rows, 0)
        scores = (
            jnp.einsum("tkgd,skd->kgts", grouped, key_block, preferred_element_type=jnp.float32)
            * query_scale
        )
        allowed = pos_block[None, :] <= query_pos[:, None]
        weights = jnp.where(allowed[None, None], jnp.exp(softcap * jnp.tanh(scores / softcap)), 0.0)
        denominator = denominator + jnp.sum(weights, axis=-1)
        numerator = numerator + jnp.einsum(
            "kgts,skd->kgtd",
            weights.astype(jnp.bfloat16),
            value_block,
            preferred_element_type=jnp.float32,
        )
        return (numerator, denominator)

    return lax.fori_loop(0, row_count // block_rows, one_block, carried)


def attend_live(carried, key_rows, value_rows, key_pos, grouped, query_pos):
    return attend(carried, key_rows, value_rows, key_pos, grouped, query_pos)


def finish(running, live_rows):
    numerator, denominator = running
    divisor = jnp.where(denominator > 0.0, denominator, 1.0)
    output = numerator / divisor[..., None]
    row_count = output.shape[2]
    output = jnp.transpose(output, (2, 0, 1, 3)).reshape(row_count, -1)
    return jnp.where(live_rows[:, None], output, 0.0).astype(jnp.bfloat16)


def body(queries, keys, values, exit_layer, tile_order):
    layer_count, row_count, q_width = queries.shape
    kv_here = keys.shape[2] // HD
    heads_here = q_width // HD
    group_size = heads_here // kv_here
    my_index = lax.axis_index(SEQ)
    first_row = my_index * row_count
    query_pos = token_positions(tile_order, first_row, row_count)
    token_exits = jnp.repeat(exit_layer, TILE, total_repeat_length=row_count)
    grouped = queries.reshape(layer_count, row_count, kv_here, group_size, HD)
    empty = (
        jnp.zeros((kv_here, group_size, row_count, HD), jnp.float32),
        jnp.zeros((kv_here, group_size, row_count), jnp.float32),
    )
    live_flags = [token_exits > 0]
    layer_id = 0
    any_live = jnp.any(live_flags[layer_id])

    def fold_one(carried, pieces, begin_at, layer_id=layer_id, any_live=any_live):
        key_pos = token_positions(tile_order, begin_at, pieces[0].shape[0])
        return attend_live(carried, pieces[0], pieces[1], key_pos, grouped[layer_id], query_pos)

    results = fold_one(
        empty, side_by_side((keys[layer_id], values[layer_id]), SEQ, 0, 1), jnp.int32(0)
    )
    attended = jnp.stack([finish(results, live_flags[0])])
    local_counts = jnp.stack([jnp.sum((exit_layer > 0).astype(jnp.int32))])
    live_tiles = by_axis(local_counts, SEQ)
    return (attended, live_tiles)


def solution(mesh):
    finer = Mesh(
        mesh.devices.reshape(mesh.shape["batch"], 2, 8, mesh.shape["head"]),
        ("batch", "seq_0", "seq_1", "head"),
    )
    return jax.shard_map(
        body,
        mesh=finer,
        in_specs=(
            P(None, BATCH_SEQ, "head"),
            P(None, BATCH_SEQ, "head"),
            P(None, BATCH_SEQ, "head"),
            P(BATCH_SEQ),
            P("batch"),
        ),
        out_specs=(P(None, BATCH_SEQ, "head"), P("batch")),
        check_vma=False,
    )
```

profile of v0, /device:TPU:1, one launch (start us, length us, event | category | flops | bytes accessed | tf_op | source)
XLA Modules:
  0.0 317.7 jit_solution(4437018939631152134)
XLA Ops:
  7.2 1.3 copy.18
  8.5 1.2 copy.19
  11.4 6.0 %psum.14 = s32[1]{0:T(128)} all-reduce(s32[1]{0:T(128)} %bitcast.11), channel_id=1, replica_groups=mesh['batch'=8,'seq_0'=2,'seq_1'=8,'head'=2] {'seq_0'}, use_global_device_ids=true, to_apply=%region_6.7 | all-reduce | flops 1 | bytes 8 | tf_op jit(solution)/shard_map/psum | solution.py:30
  17.4 13.9 %psum.15 = s32[1]{0:T(128)} all-reduce(s32[1]{0:T(128)} %psum.14), channel_id=1, replica_groups=mesh['batch'=8,'seq_0'=2,'seq_1'=8,'head'=2] {'seq_1'}, use_global_device_ids=true, to_apply=%region_7.8 | all-reduce | flops 1 | bytes 8 | tf_op jit(solution)/shard_map/psum | solution.py:30
  32.6 1.9 fusion.35
  35.0 168.8 %all-gather.2.cloned.1.call-done = bf16[6144,1024]{0,1:T(8,128)(2,1)} async-done(((bf16[384,1024]{0,1:T(8,128)(2,1)}), bf16[6144,1024]{0,1:T(8,128)(2,1)}) %all-gather.2.cloned.1.call-update) | async-done | bytes 12582928 | tf_op jit(solution)/shard_map/all_gather | solution.py:21
  203.8 10.6 %fusion.38 = (bf16[6144,512]{0,1:T(8,128)(2,1)}, bf16[6144,512]{0,1:T(8,128)(2,1)}) fusion(bf16[6144,1024]{0,1:T(8,128)(2,1)} %all-gather.2.cloned.1.call-done), kind=kLoop, calls=%fused_computation.65 | loop fusion | bytes 25165824 | tf_op jit(solution)/shard_map/slice | solution.py:23
  214.4 93.7 %while.19 = (s32[]{:T(128)}, f32[2,2,384,256]{3,2,1,0:T(8,128)S(1)}, f32[2,2,384]{2,1,0:T(2,128)S(1)}, s32[6144]{0:T(1024)S(1)}, s32[384]{0:T(512)S(1)}, /*index...) while((s32[]{:T(128)}, ...), condition=%wide.region_4.5_spmd.clone, body=%wide.region_2.4_spmd.clone.sunk | while | flops 812582400 | bytes 11894458 | solution.py:73
  214.7 3.9 %fusion.48 = (f32[2,2,384]{2,1,0:T(2,128)S(1)}, f32[2,512,384,2]{2,1,3,0:T(8,128)}) fusion(pred[384,512]{0,1:T(8,128)(4,1)S(1)} %broadcast_compare_fusion.2, bf16[384,2,2,256]{3,0,2,1:T(8,128)(2,1)S(1)} %get-tuple-element.366, bf16[6144,2,256]{0,2,1:T(8,128)(2,1)} %get-tuple-element.365, s32[]{:T(128)S(6)} %select_n.150), kind=kOutput, calls=%fused_computation.1.clone.1 | convolution fusion | flops 405797376 | bytes 4659204 | tf_op jit(solution)/shard_map/while/body/eval_jaxpr/tkgd,skd->kgts/dot_general | solution.py:59
  218.6 3.6 %select_add_fusion.4 = f32[2,2,384,256]{3,2,1,0:T(8,128)S(1)} fusion(f32[2,2,384,256]{3,2,1,0:T(8,128)S(1)} %get-tuple-element.349, f32[2,512,384,2]{2,1,3,0:T(8,128)} %get-tuple-element.334, pred[384,512]{0,1:T(8,128)(4,1)S(1)} %broadcast_compare_fusion.2, pred[]{:T(512)S(6)} %compare.35, bf16[6144,2,256]{0,2,1:T(8,128)(2,1)} %get-tuple-element.367, ...), kind=kOutput, calls=%fused_computation.4.clone.1 | convolution fusion | flops 406585344 | bytes 7012357 | tf_op jit(solution)/shard_map/while/body/eval_jaxpr/kgts,skd->kgtd/dot_general | solution.py:65
  222.5 3.9 %fusion.48 = (f32[2,2,384]{2,1,0:T(2,128)S(1)}, f32[2,512,384,2]{2,1,3,0:T(8,128)}) fusion(pred[384,512]{0,1:T(8,128)(4,1)S(1)} %broadcast_compare_fusion.2, bf16[384,2,2,256]{3,0,2,1:T(8,128)(2,1)S(1)} %get-tuple-element.366, bf16[6144,2,256]{0,2,1:T(8,128)(2,1)} %get-tuple-element.365, s32[]{:T(128)S(6)} %select_n.150), kind=kOutput, calls=%fused_computation.1.clone.1 | convolution fusion | flops 405797376 | bytes 4659204 | tf_op jit(solution)/shard_map/while/body/eval_jaxpr/tkgd,skd->kgts/dot_general | solution.py:59
  226.4 3.6 %select_add_fusion.4 = f32[2,2,384,256]{3,2,1,0:T(8,128)S(1)} fusion(f32[2,2,384,256]{3,2,1,0:T(8,128)S(1)} %get-tuple-element.349, f32[2,512,384,2]{2,1,3,0:T(8,128)} %get-tuple-element.334, pred[384,512]{0,1:T(8,128)(4,1)S(1)} %broadcast_compare_fusion.2, pred[]{:T(512)S(6)} %compare.35, bf16[6144,2,256]{0,2,1:T(8,128)(2,1)} %get-tuple-element.367, ...), kind=kOutput, calls=%fused_computation.4.clone.1 | convolution fusion | flops 406585344 | bytes 7012357 | tf_op jit(solution)/shard_map/while/body/eval_jaxpr/kgts,skd->kgtd/dot_general | solution.py:65
  230.3 3.9 %fusion.48 = (f32[2,2,384]{2,1,0:T(2,128)S(1)}, f32[2,512,384,2]{2,1,3,0:T(8,128)}) fusion(pred[384,512]{0,1:T(8,128)(4,1)S(1)} %broadcast_compare_fusion.2, bf16[384,2,2,256]{3,0,2,1:T(8,128)(2,1)S(1)} %get-tuple-element.366, bf16[6144,2,256]{0,2,1:T(8,128)(2,1)} %get-tuple-element.365, s32[]{:T(128)S(6)} %select_n.150), kind=kOutput, calls=%fused_computation.1.clone.1 | convolution fusion | flops 405797376 | bytes 4659204 | tf_op jit(solution)/shard_map/while/body/eval_jaxpr/tkgd,skd->kgts/dot_general | solution.py:59
  234.2 3.6 %select_add_fusion.4 = f32[2,2,384,256]{3,2,1,0:T(8,128)S(1)} fusion(f32[2,2,384,256]{3,2,1,0:T(8,128)S(1)} %get-tuple-element.349, f32[2,512,384,2]{2,1,3,0:T(8,128)} %get-tuple-element.334, pred[384,512]{0,1:T(8,128)(4,1)S(1)} %broadcast_compare_fusion.2, pred[]{:T(512)S(6)} %compare.35, bf16[6144,2,256]{0,2,1:T(8,128)(2,1)} %get-tuple-element.367, ...), kind=kOutput, calls=%fused_computation.4.clone.1 | convolution fusion | flops 406585344 | bytes 7012357 | tf_op jit(solution)/shard_map/while/body/eval_jaxpr/kgts,skd->kgtd/dot_general | solution.py:65
  238.1 3.9 %fusion.48 = (f32[2,2,384]{2,1,0:T(2,128)S(1)}, f32[2,512,384,2]{2,1,3,0:T(8,128)}) fusion(pred[384,512]{0,1:T(8,128)(4,1)S(1)} %broadcast_compare_fusion.2, bf16[384,2,2,256]{3,0,2,1:T(8,128)(2,1)S(1)} %get-tuple-element.366, bf16[6144,2,256]{0,2,1:T(8,128)(2,1)} %get-tuple-element.365, s32[]{:T(128)S(6)} %select_n.150), kind=kOutput, calls=%fused_computation.1.clone.1 | convolution fusion | flops 405797376 | bytes 4659204 | tf_op jit(solution)/shard_map/while/body/eval_jaxpr/tkgd,skd->kgts/dot_general | solution.py:59
  242.0 3.6 %select_add_fusion.4 = f32[2,2,384,256]{3,2,1,0:T(8,128)S(1)} fusion(f32[2,2,384,256]{3,2,1,0:T(8,128)S(1)} %get-tuple-element.349, f32[2,512,384,2]{2,1,3,0:T(8,128)} %get-tuple-element.334, pred[384,512]{0,1:T(8,128)(4,1)S(1)} %broadcast_compare_fusion.2, pred[]{:T(512)S(6)} %compare.35, bf16[6144,2,256]{0,2,1:T(8,128)(2,1)} %get-tuple-element.367, ...), kind=kOutput, calls=%fused_computation.4.clone.1 | convolution fusion | flops 406585344 | bytes 7012357 | tf_op jit(solution)/shard_map/while/body/eval_jaxpr/kgts,skd->kgtd/dot_general | solution.py:65
  245.9 3.9 %fusion.48 = (f32[2,2,384]{2,1,0:T(2,128)S(1)}, f32[2,512,384,2]{2,1,3,0:T(8,128)}) fusion(pred[384,512]{0,1:T(8,128)(4,1)S(1)} %broadcast_compare_fusion.2, bf16[384,2,2,256]{3,0,2,1:T(8,128)(2,1)S(1)} %get-tuple-element.366, bf16[6144,2,256]{0,2,1:T(8,128)(2,1)} %get-tuple-element.365, s32[]{:T(128)S(6)} %select_n.150), kind=kOutput, calls=%fused_computation.1.clone.1 | convolution fusion | flops 405797376 | bytes 4659204 | tf_op jit(solution)/shard_map/while/body/eval_jaxpr/tkgd,skd->kgts/dot_general | solution.py:59
  249.9 3.6 %select_add_fusion.4 = f32[2,2,384,256]{3,2,1,0:T(8,128)S(1)} fusion(f32[2,2,384,256]{3,2,1,0:T(8,128)S(1)} %get-tuple-element.349, f32[2,512,384,2]{2,1,3,0:T(8,128)} %get-tuple-element.334, pred[384,512]{0,1:T(8,128)(4,1)S(1)} %broadcast_compare_fusion.2, pred[]{:T(512)S(6)} %compare.35, bf16[6144,2,256]{0,2,1:T(8,128)(2,1)} %get-tuple-element.367, ...), kind=kOutput, calls=%fused_computation.4.clone.1 | convolution fusion | flops 406585344 | bytes 7012357 | tf_op jit(solution)/shard_map/while/body/eval_jaxpr/kgts,skd->kgtd/dot_general | solution.py:65
  253.7 3.9 %fusion.48 = (f32[2,2,384]{2,1,0:T(2,128)S(1)}, f32[2,512,384,2]{2,1,3,0:T(8,128)}) fusion(pred[384,512]{0,1:T(8,128)(4,1)S(1)} %broadcast_compare_fusion.2, bf16[384,2,2,256]{3,0,2,1:T(8,128)(2,1)S(1)} %get-tuple-element.366, bf16[6144,2,256]{0,2,1:T(8,128)(2,1)} %get-tuple-element.365, s32[]{:T(128)S(6)} %select_n.150), kind=kOutput, calls=%fused_computation.1.clone.1 | convolution fusion | flops 405797376 | bytes 4659204 | tf_op jit(solution)/shard_map/while/body/eval_jaxpr/tkgd,skd->kgts/dot_general | solution.py:59
  257.7 3.6 %select_add_fusion.4 = f32[2,2,384,256]{3,2,1,0:T(8,128)S(1)} fusion(f32[2,2,384,256]{3,2,1,0:T(8,128)S(1)} %get-tuple-element.349, f32[2,512,384,2]{2,1,3,0:T(8,128)} %get-tuple-element.334, pred[384,512]{0,1:T(8,128)(4,1)S(1)} %broadcast_compare_fusion.2, pred[]{:T(512)S(6)} %compare.35, bf16[6144,2,256]{0,2,1:T(8,128)(2,1)} %get-tuple-element.367, ...), kind=kOutput, calls=%fused_computation.4.clone.1 | convolution fusion | flops 406585344 | bytes 7012357 | tf_op jit(solution)/shard_map/while/body/eval_jaxpr/kgts,skd->kgtd/dot_general | solution.py:65
  261.5 3.9 %fusion.48 = (f32[2,2,384]{2,1,0:T(2,128)S(1)}, f32[2,512,384,2]{2,1,3,0:T(8,128)}) fusion(pred[384,512]{0,1:T(8,128)(4,1)S(1)} %broadcast_compare_fusion.2, bf16[384,2,2,256]{3,0,2,1:T(8,128)(2,1)S(1)} %get-tuple-element.366, bf16[6144,2,256]{0,2,1:T(8,128)(2,1)} %get-tuple-element.365, s32[]{:T(128)S(6)} %select_n.150), kind=kOutput, calls=%fused_computation.1.clone.1 | convolution fusion | flops 405797376 | bytes 4659204 | tf_op jit(solution)/shard_map/while/body/eval_jaxpr/tkgd,skd->kgts/dot_general | solution.py:59
  265.5 3.6 %select_add_fusion.4 = f32[2,2,384,256]{3,2,1,0:T(8,128)S(1)} fusion(f32[2,2,384,256]{3,2,1,0:T(8,128)S(1)} %get-tuple-element.349, f32[2,512,384,2]{2,1,3,0:T(8,128)} %get-tuple-element.334, pred[384,512]{0,1:T(8,128)(4,1)S(1)} %broadcast_compare_fusion.2, pred[]{:T(512)S(6)} %compare.35, bf16[6144,2,256]{0,2,1:T(8,128)(2,1)} %get-tuple-element.367, ...), kind=kOutput, calls=%fused_computation.4.clone.1 | convolution fusion | flops 406585344 | bytes 7012357 | tf_op jit(solution)/shard_map/while/body/eval_jaxpr/kgts,skd->kgtd/dot_general | solution.py:65
  269.3 3.9 %fusion.48 = (f32[2,2,384]{2,1,0:T(2,128)S(1)}, f32[2,512,384,2]{2,1,3,0:T(8,128)}) fusion(pred[384,512]{0,1:T(8,128)(4,1)S(1)} %broadcast_compare_fusion.2, bf16[384,2,2,256]{3,0,2,1:T(8,128)(2,1)S(1)} %get-tuple-element.366, bf16[6144,2,256]{0,2,1:T(8,128)(2,1)} %get-tuple-element.365, s32[]{:T(128)S(6)} %select_n.150), kind=kOutput, calls=%fused_computation.1.clone.1 | convolution fusion | flops 405797376 | bytes 4659204 | tf_op jit(solution)/shard_map/while/body/eval_jaxpr/tkgd,skd->kgts/dot_general | solution.py:59
  273.3 3.6 %select_add_fusion.4 = f32[2,2,384,256]{3,2,1,0:T(8,128)S(1)} fusion(f32[2,2,384,256]{3,2,1,0:T(8,128)S(1)} %get-tuple-element.349, f32[2,512,384,2]{2,1,3,0:T(8,128)} %get-tuple-element.334, pred[384,512]{0,1:T(8,128)(4,1)S(1)} %broadcast_compare_fusion.2, pred[]{:T(512)S(6)} %compare.35, bf16[6144,2,256]{0,2,1:T(8,128)(2,1)} %get-tuple-element.367, ...), kind=kOutput, calls=%fused_computation.4.clone.1 | convolution fusion | flops 406585344 | bytes 7012357 | tf_op jit(solution)/shard_map/while/body/eval_jaxpr/kgts,skd->kgtd/dot_general | solution.py:65
  277.1 3.9 %fusion.48 = (f32[2,2,384]{2,1,0:T(2,128)S(1)}, f32[2,512,384,2]{2,1,3,0:T(8,128)}) fusion(pred[384,512]{0,1:T(8,128)(4,1)S(1)} %broadcast_compare_fusion.2, bf16[384,2,2,256]{3,0,2,1:T(8,128)(2,1)S(1)} %get-tuple-element.366, bf16[6144,2,256]{0,2,1:T(8,128)(2,1)} %get-tuple-element.365, s32[]{:T(128)S(6)} %select_n.150), kind=kOutput, calls=%fused_computation.1.clone.1 | convolution fusion | flops 405797376 | bytes 4659204 | tf_op jit(solution)/shard_map/while/body/eval_jaxpr/tkgd,skd->kgts/dot_general | solution.py:59
  281.1 3.6 %select_add_fusion.4 = f32[2,2,384,256]{3,2,1,0:T(8,128)S(1)} fusion(f32[2,2,384,256]{3,2,1,0:T(8,128)S(1)} %get-tuple-element.349, f32[2,512,384,2]{2,1,3,0:T(8,128)} %get-tuple-element.334, pred[384,512]{0,1:T(8,128)(4,1)S(1)} %broadcast_compare_fusion.2, pred[]{:T(512)S(6)} %compare.35, bf16[6144,2,256]{0,2,1:T(8,128)(2,1)} %get-tuple-element.367, ...), kind=kOutput, calls=%fused_computation.4.clone.1 | convolution fusion | flops 406585344 | bytes 7012357 | tf_op jit(solution)/shard_map/while/body/eval_jaxpr/kgts,skd->kgtd/dot_general | solution.py:65
  284.9 3.9 %fusion.48 = (f32[2,2,384]{2,1,0:T(2,128)S(1)}, f32[2,512,384,2]{2,1,3,0:T(8,128)}) fusion(pred[384,512]{0,1:T(8,128)(4,1)S(1)} %broadcast_compare_fusion.2, bf16[384,2,2,256]{3,0,2,1:T(8,128)(2,1)S(1)} %get-tuple-element.366, bf16[6144,2,256]{0,2,1:T(8,128)(2,1)} %get-tuple-element.365, s32[]{:T(128)S(6)} %select_n.150), kind=kOutput, calls=%fused_computation.1.clone.1 | convolution fusion | flops 405797376 | bytes 4659204 | tf_op jit(solution)/shard_map/while/body/eval_jaxpr/tkgd,skd->kgts/dot_general | solution.py:59
  288.9 3.6 %select_add_fusion.4 = f32[2,2,384,256]{3,2,1,0:T(8,128)S(1)} fusion(f32[2,2,384,256]{3,2,1,0:T(8,128)S(1)} %get-tuple-element.349, f32[2,512,384,2]{2,1,3,0:T(8,128)} %get-tuple-element.334, pred[384,512]{0,1:T(8,128)(4,1)S(1)} %broadcast_compare_fusion.2, pred[]{:T(512)S(6)} %compare.35, bf16[6144,2,256]{0,2,1:T(8,128)(2,1)} %get-tuple-element.367, ...), kind=kOutput, calls=%fused_computation.4.clone.1 | convolution fusion | flops 406585344 | bytes 7012357 | tf_op jit(solution)/shard_map/while/body/eval_jaxpr/kgts,skd->kgtd/dot_general | solution.py:65
  292.7 3.9 %fusion.48 = (f32[2,2,384]{2,1,0:T(2,128)S(1)}, f32[2,512,384,2]{2,1,3,0:T(8,128)}) fusion(pred[384,512]{0,1:T(8,128)(4,1)S(1)} %broadcast_compare_fusion.2, bf16[384,2,2,256]{3,0,2,1:T(8,128)(2,1)S(1)} %get-tuple-element.366, bf16[6144,2,256]{0,2,1:T(8,128)(2,1)} %get-tuple-element.365, s32[]{:T(128)S(6)} %select_n.150), kind=kOutput, calls=%fused_computation.1.clone.1 | convolution fusion | flops 405797376 | bytes 4659204 | tf_op jit(solution)/shard_map/while/body/eval_jaxpr/tkgd,skd->kgts/dot_general | solution.py:59
  296.7 3.6 %select_add_fusion.4 = f32[2,2,384,256]{3,2,1,0:T(8,128)S(1)} fusion(f32[2,2,384,256]{3,2,1,0:T(8,128)S(1)} %get-tuple-element.349, f32[2,512,384,2]{2,1,3,0:T(8,128)} %get-tuple-element.334, pred[384,512]{0,1:T(8,128)(4,1)S(1)} %broadcast_compare_fusion.2, pred[]{:T(512)S(6)} %compare.35, bf16[6144,2,256]{0,2,1:T(8,128)(2,1)} %get-tuple-element.367, ...), kind=kOutput, calls=%fused_computation.4.clone.1 | convolution fusion | flops 406585344 | bytes 7012357 | tf_op jit(solution)/shard_map/while/body/eval_jaxpr/kgts,skd->kgtd/dot_general | solution.py:65
  300.6 3.9 %fusion.48 = (f32[2,2,384]{2,1,0:T(2,128)S(1)}, f32[2,512,384,2]{2,1,3,0:T(8,128)}) fusion(pred[384,512]{0,1:T(8,128)(4,1)S(1)} %broadcast_compare_fusion.2, bf16[384,2,2,256]{3,0,2,1:T(8,128)(2,1)S(1)} %get-tuple-element.366, bf16[6144,2,256]{0,2,1:T(8,128)(2,1)} %get-tuple-element.365, s32[]{:T(128)S(6)} %select_n.150), kind=kOutput, calls=%fused_computation.1.clone.1 | convolution fusion | flops 405797376 | bytes 4659204 | tf_op jit(solution)/shard_map/while/body/eval_jaxpr/tkgd,skd->kgts/dot_general | solution.py:59
  304.5 3.6 %select_add_fusion.4 = f32[2,2,384,256]{3,2,1,0:T(8,128)S(1)} fusion(f32[2,2,384,256]{3,2,1,0:T(8,128)S(1)} %get-tuple-element.349, f32[2,512,384,2]{2,1,3,0:T(8,128)} %get-tuple-element.334, pred[384,512]{0,1:T(8,128)(4,1)S(1)} %broadcast_compare_fusion.2, pred[]{:T(512)S(6)} %compare.35, bf16[6144,2,256]{0,2,1:T(8,128)(2,1)} %get-tuple-element.367, ...), kind=kOutput, calls=%fused_computation.4.clone.1 | convolution fusion | flops 406585344 | bytes 7012357 | tf_op jit(solution)/shard_map/while/body/eval_jaxpr/kgts,skd->kgtd/dot_general | solution.py:65
  (64 shorter events, 9.3 us)
Async XLA Ops:
  7.2 3.6 %copy-start.1 = (s32[3]{0:T(128)S(1)}, s32[3]{0:T(128)}, u32[]{:S(2)}) copy-start(s32[3]{0:T(128)} %param.12) | copy-start | bytes 40
  7.2 24.1 %copy-start = (bf16[1,384,1024]{2,1,0:T(8,128)(2,1)S(1)}, bf16[1,384,1024]{2,1,0:T(8,128)(2,1)}, u32[]{:S(2)}) copy-start(bf16[1,384,1024]{2,1,0:T(8,128)(2,1)} %param.9) | copy-start | bytes 2359300
  7.2 196.6 %all-gather.2.cloned.1.call-start = ((), (), s32[]{:S(2)}) async-start(), calls=%async_computation | async-start | bytes 13369344 | tf_op jit(solution)/shard_map/all_gather | solution.py:21
  8.5 26.0 %copy-start.2 = (s32[48]{0:T(128)S(1)}, s32[48]{0:T(128)}, u32[]{:S(2)}) copy-start(s32[48]{0:T(128)} %param.13) | copy-start | bytes 580
Sparse Core Ops, SparseCore 0:
  11.0 192.7 all-gather.1
where the time goes:
time: 321 us; the launch traced here: 318 us
  waiting for transfers between devices  169 us (53%)
  matrix products  90 us (28%)
  blocking collectives  19.9 us (6%)
  local copies, waits for them, and re-layouts  16.7 us (5%)
  between operations  14.2 us (4%)
  other arithmetic  7.52 us (2%)
    all_gather x1, waiting for transfers between devices, side_by_side(): lax.all_gather(both, axis, axis=dim, tiled=True)  169 us
    dot_general x12, matrix products, one_block(): jnp.einsum('tkgd,skd->kgts', grouped, key_block, preferred_element_type=j...  47.3 us
    dot_general x12, matrix products, one_block(): jnp.einsum('kgts,skd->kgtd', weights.astype(jnp.bfloat16), value_block, p...  42.7 us
    psum x2, blocking collectives, by_axis(): x = lax.psum(x, axis)  19.9 us
    slice x1, local copies, waits for them, and re-layouts, side_by_side(): lax.slice_in_dim(whole, at, at + a.shape[along], axis=along)  10.6 us
  transfers between devices with their start and end apart: 1, of which 1 were waited for; matrix products, arithmetic and copies ran while one was open for 1% of the time, Pallas kernels for 0%

commit v1 on v0

v1 whole, which is shorter than its diff:
```python
import math

import jax
import jax.numpy as jnp
from jax import lax
from jax.experimental import pallas as pl
from jax.experimental.pallas import tpu as pltpu
from jax.sharding import PartitionSpec as P

MESH = pl.DeviceIdType.MESH
HD = 256
TILE = 128
ROWS = 384
OWN_TILES = 3
Z = 8
SEQ = 16
PAIRS = 12
OWN_SLOT = (1, 22, 0)
SCORE_TO_TANH = 0.0625 / 50.0
TANH_TO_EXP2 = 50.0 * math.log2(math.e)


def kernel(
    q_hbm, k_hbm, v_hbm, exit_ref, order_ref,
    out_ref, live_ref,
    q, kv, acc, den, q_relay, o_send, o_relay, o_back, d_send, d_relay, d_back, counts,
    ld_q, ld_kv, z_out, z_in, q_out, q_in, o_out, o_in, c_out, c_in,
):
    batch = lax.axis_index("batch")
    seq = lax.axis_index("seq")
    y_lo = lax.rem(batch, 2)
    y_hi = seq // Z
    z = lax.rem(seq, Z)
    other_batch = batch + 1 - 2 * y_lo
    up = {"seq": y_hi * Z + lax.rem(z + 1, Z)}
    down = {"seq": y_hi * Z + lax.rem(z + Z - 1, Z)}
    y_up = {"batch": other_batch, "seq": lax.rem(y_hi + y_lo, 2) * Z + z}
    y_down = {"batch": other_batch, "seq": lax.rem(y_hi + 1 - y_lo, 2) * Z + z}
    z_to = (up, down)
    y_to = (y_up, y_down)

    def rows(t):
        return pl.ds(t * TILE, TILE)

    loads_kv = {}
    for h in range(2):
        for t in range(OWN_TILES):
            for which, src in ((0, k_hbm), (1, v_hbm)):
                loads_kv[h, t, which] = pltpu.make_async_copy(
                    src.at[rows(t), pl.ds(h * HD, HD)],
                    kv.at[h, which, OWN_SLOT[t]],
                    ld_kv.at[h, t, which],
                )
    loads_q = [
        pltpu.make_async_copy(q_hbm.at[:, pl.ds(n * HD, HD)], q.at[0, n], ld_q.at[n])
        for n in range(4)
    ]
    for t in range(OWN_TILES):
        for which in range(2):
            loads_kv[0, t, which].start()
    for n in range(4):
        loads_q[n].start()
    for t in range(OWN_TILES):
        for which in range(2):
            loads_kv[1, t, which].start()

    barrier = pltpu.get_barrier_semaphore()

    def greet(n, c):
        pl.semaphore_signal(
            barrier, inc=1, device_id={"seq": lax.rem(seq + n, SEQ)}, device_id_type=MESH
        )
        return c

    for peer in y_to:
        pl.semaphore_signal(barrier, inc=1, device_id=peer, device_id_type=MESH)
    lax.fori_loop(1, SEQ, greet, 0)

    local_live = jnp.int32(0)
    for t in range(OWN_TILES):
        local_live = local_live + (exit_ref[t] > 0).astype(jnp.int32)
    counts[seq] = jnp.full((8, 128), local_live, jnp.int32)

    pl.semaphore_wait(barrier, SEQ + 1)

    def z_copy(way, h, src_slot, i):
        dst_slot = 2 * (i + 1) + (i // 10 if way == 0 else 1)
        return pltpu.make_async_remote_copy(
            src_ref=kv.at[h, :, src_slot],
            dst_ref=kv.at[h, :, dst_slot],
            send_sem=z_out.at[way, h, i],
            recv_sem=z_in.at[way, h, i],
            device_id=z_to[way],
            device_id_type=MESH,
        )

    def z_slot(way, i):
        return 2 * (i + 1) + (i // 10 if way == 0 else 1)

    def q_first(way, g, t):
        return pltpu.make_async_remote_copy(
            src_ref=q.at[0, 2 * g + way, rows(t)],
            dst_ref=q_relay.at[way, g, t],
            send_sem=q_out.at[0, way, g, t],
            recv_sem=q_in.at[0, way, g, t],
            device_id=y_to[way],
            device_id_type=MESH,
        )

    def q_second(way, g, t):
        return pltpu.make_async_remote_copy(
            src_ref=q_relay.at[way, g, t],
            dst_ref=q.at[1, 2 * g + way, rows(t)],
            send_sem=q_out.at[1, way, g, t],
            recv_sem=q_in.at[1, way, g, t],
            device_id=y_to[way],
            device_id_type=MESH,
        )

    def o_first(way, g, t):
        n = 2 * g + way
        src, dst = (
            (o_send.at[n, rows(t)], o_relay.at[way, g, t])
            if t < OWN_TILES
            else (d_send.at[n], d_relay.at[n])
        )
        return pltpu.make_async_remote_copy(
            src_ref=src,
            dst_ref=dst,
            send_sem=o_out.at[0, way, g, t],
            recv_sem=o_in.at[0, way, g, t],
            device_id=y_to[way],
            device_id_type=MESH,
        )

    def o_second(way, g, t):
        n = 2 * g + way
        src, dst = (
            (o_relay.at[way, g, t], o_back.at[n, rows(t)])
            if t < OWN_TILES
            else (d_relay.at[n], d_back.at[n])
        )
        return pltpu.make_async_remote_copy(
            src_ref=src,
            dst_ref=dst,
            send_sem=o_out.at[1, way, g, t],
            recv_sem=o_in.at[1, way, g, t],
            device_id=y_to[way],
            device_id_type=MESH,
        )

    def send_own(h, j):
        for way in range(2):
            z_copy(way, h, OWN_SLOT[j if way == 0 else 2 - j], j).start()

    for t in (0, 2, 1):
        for which in range(2):
            loads_kv[0, t, which].wait()
    for j in range(OWN_TILES):
        send_own(0, j)
    for n in range(4):
        loads_q[n].wait()
    for t in range(OWN_TILES):
        for way in range(2):
            q_first(way, 0, t).start()

    def count_copy(n):
        return pltpu.make_async_remote_copy(
            src_ref=counts.at[seq],
            dst_ref=counts.at[seq],
            send_sem=c_out.at[n],
            recv_sem=c_in.at[n],
            device_id={"seq": lax.rem(seq + n, SEQ)},
            device_id_type=MESH,
        )

    def send_count(n, c):
        count_copy(n).start()
        return c

    lax.fori_loop(1, SEQ, send_count, 0)

    for t in range(OWN_TILES):
        for which in range(2):
            loads_kv[1, t, which].wait()

    acc[...] = jnp.zeros_like(acc)
    den[...] = jnp.zeros_like(den)

    ahead = lax.broadcasted_iota(jnp.int32, (TILE, TILE), 1) - lax.broadcasted_iota(
        jnp.int32, (TILE, TILE), 0
    )

    def work(src, h, p):
        column = lax.rem(y_hi + src, 2)
        away = (p + 2) // 3
        t0 = lax.rem(p + 2, 3)
        away_low = jnp.where(p == PAIRS - 1, 0, away)
        k_tiles = (
            (y_hi * Z + lax.rem(z + Z - away_low, Z)) * OWN_TILES + t0,
            (y_hi * Z + lax.rem(z + away, Z)) * OWN_TILES + 2 - t0,
        )
        query = q[src, pl.ds(2 * h, 2)].reshape(2 * ROWS, HD)
        key = kv[h, 0, pl.ds(2 * p, 2)].reshape(2 * TILE, HD)
        value = kv[h, 1, pl.ds(2 * p, 2)].reshape(2 * TILE, HD)
        score = lax.dot_general(
            query, key, (((1,), (1,)), ((), ())), preferred_element_type=jnp.float32
        )
        weight = jnp.exp2(jnp.tanh(score * SCORE_TO_TANH) * TANH_TO_EXP2)
        k_order = [order_ref[n] for n in k_tiles]
        masks = []
        for t in range(OWN_TILES):
            q_order = order_ref[(column * Z + z) * OWN_TILES + t]
            masks.append([ahead <= (q_order - k) * TILE for k in k_order])
        blocks = []
        for head in range(2):
            for t in range(OWN_TILES):
                lower = (head * OWN_TILES + t) * TILE
                both = weight[lower : lower + TILE]
                left = jnp.where(masks[t][0], both[:, :TILE], 0.0)
                right = jnp.where(masks[t][1], both[:, TILE:], 0.0)
                den[src, 2 * h + head, rows(t)] += left + right
                blocks.append(jnp.concatenate([left, right], axis=1).astype(jnp.bfloat16))
        product = jnp.dot(
            jnp.concatenate(blocks, axis=0), value, preferred_element_type=jnp.float32
        )
        acc[src, pl.ds(2 * h, 2)] += product.reshape(2, ROWS, HD)

    def give_back(g):
        for way in range(2):
            n = 2 * g + way
            for t in range(OWN_TILES):
                o_send[n, rows(t)] = acc[1, n, rows(t)].astype(jnp.bfloat16)
                o_first(way, g, t).start()
        for way in range(2):
            n = 2 * g + way
            for t in range(OWN_TILES):
                total = jnp.sum(jnp.transpose(den[1, n, rows(t)]), axis=0, keepdims=True)
                d_send[n, :, rows(t)] = jnp.broadcast_to(total, (8, TILE))
            o_first(way, g, OWN_TILES).start()

    def step(u, c):
        h = u // PAIRS
        p = lax.rem(u, PAIRS)
        i = p - 1

        @pl.when((p >= 1) & (p <= PAIRS - 2))
        def _():
            for way in range(2):
                z_copy(way, h, 0, i).wait_recv()

                @pl.when(i + 3 <= (10 - h if way == 0 else 9 + h))
                def _():
                    z_copy(way, h, z_slot(way, i), i + 3).start()

        for way in range(2):

            @pl.when((p == PAIRS - 1) & (h == way))
            def _():
                z_copy(way, way, 0, 10).wait_recv()

        for j in range(OWN_TILES):

            @pl.when(u == 6 + j)
            def _():
                send_own(1, j)

        @pl.when(u == 1)
        def _():
            for t in range(OWN_TILES):
                for way in range(2):
                    q_first(way, 0, t).wait_recv()
                    q_second(way, 0, t).start()
            for t in range(OWN_TILES):
                for way in range(2):
                    q_first(way, 1, t).start()

        @pl.when(u == 3)
        def _():
            for t in range(OWN_TILES):
                for way in range(2):
                    q_first(way, 1, t).wait_recv()
                    q_second(way, 1, t).start()

        for g, at in ((0, 5), (1, PAIRS)):

            @pl.when(u == at)
            def _():
                for t in range(OWN_TILES):
                    for way in range(2):
                        q_second(way, g, t).wait_recv()

        @pl.when(u == PAIRS + 3)
        def _():
            for t in range(OWN_TILES + 1):
                for way in range(2):
                    o_first(way, 0, t).wait_recv()
                    o_second(way, 0, t).start()

        @pl.when(u < 2 * PAIRS - 1)
        def _():
            work(0, h, p)

        first = jnp.where(u < 5, 0, jnp.where(u < 10, 2 * (u - 5), u))
        many = jnp.where(u < 5, 0, jnp.where(u < 10, 2, 1))

        def remote(n, c):
            work(1, (first + n) // PAIRS, lax.rem(first + n, PAIRS))
            return c

        lax.fori_loop(0, many, remote, 0)

        @pl.when(u == PAIRS - 1)
        def _():
            give_back(0)

        return c

    lax.fori_loop(0, 2 * PAIRS, step, 0)
    give_back(1)
    work(0, 1, PAIRS - 1)

    def wait_count(n, c):
        count_copy(n).wait_recv()
        return c

    lax.fori_loop(1, SEQ, wait_count, 0)
    total = counts[0]
    for n in range(1, SEQ):
        total = total + counts[n]
    live_ref[...] = total

    def finish(g):
        for way in range(2):
            n = 2 * g + way
            o_second(way, g, OWN_TILES).wait_recv()
            for t in range(OWN_TILES):
                o_second(way, g, t).wait_recv()
                mine = jnp.sum(den[0, n, rows(t)], axis=1, keepdims=True)
                theirs = jnp.transpose(
                    jnp.broadcast_to(d_back[n, 0:1, rows(t)], (TILE, TILE))
                )
                inverse = 1.0 / (theirs + mine)
                alive = jnp.full((TILE, TILE), exit_ref[t], jnp.int32) > 0
                for half in range(2):
                    lanes = pl.ds(half * TILE, TILE)
                    top = acc[0, n, rows(t), lanes] + o_back[n, rows(t), lanes].astype(
                        jnp.float32
                    )
                    out_ref[rows(t), pl.ds(n * HD + half * TILE, TILE)] = jnp.where(
                        alive, top * inverse, 0.0
                    ).astype(jnp.bfloat16)

    finish(0)
    for t in range(OWN_TILES + 1):
        for way in range(2):
            o_first(way, 1, t).wait_recv()
            o_second(way, 1, t).start()
    finish(1)

    for way in range(2):
        for h in range(2):

            def z_sent(i, c):
                z_copy(way, h, 0, i).wait_send()
                return c

            lax.fori_loop(0, 11 if way == h else 10, z_sent, 0)
        for g in range(2):
            for t in range(OWN_TILES):
                q_first(way, g, t).wait_send()
                q_second(way, g, t).wait_send()
            for t in range(OWN_TILES + 1):
                o_first(way, g, t).wait_send()
                o_second(way, g, t).wait_send()

    def count_sent(n, c):
        count_copy(n).wait_send()
        return c

    lax.fori_loop(1, SEQ, count_sent, 0)


def body(queries, keys, values, exit_layer, tile_order):
    hbm = pl.BlockSpec(memory_space=pltpu.HBM)
    smem = pl.BlockSpec(memory_space=pltpu.SMEM)
    vmem = pl.BlockSpec(memory_space=pltpu.VMEM)
    bf16, f32 = jnp.bfloat16, jnp.float32
    dma = pltpu.SemaphoreType.DMA
    attended, live = pl.pallas_call(
        kernel,
        out_shape=(
            jax.ShapeDtypeStruct((ROWS, 4 * HD), bf16),
            jax.ShapeDtypeStruct((8, 128), jnp.int32),
        ),
        in_specs=[hbm, hbm, hbm, smem, smem],
        out_specs=(vmem, vmem),
        scratch_shapes=[
            pltpu.VMEM((2, 4, ROWS, HD), bf16),
            pltpu.VMEM((2, 2, 2 * PAIRS, TILE, HD), bf16),
            pltpu.VMEM((2, 4, ROWS, HD), f32),
            pltpu.VMEM((2, 4, ROWS, TILE), f32),
            pltpu.VMEM((2, 2, OWN_TILES, TILE, HD), bf16),
            pltpu.VMEM((4, ROWS, HD), bf16),
            pltpu.VMEM((2, 2, OWN_TILES, TILE, HD), bf16),
            pltpu.VMEM((4, ROWS, HD), bf16),
            pltpu.VMEM((4, 8, ROWS), f32),
            pltpu.VMEM((4, 8, ROWS), f32),
            pltpu.VMEM((4, 8, ROWS), f32),
            pltpu.VMEM((SEQ, 8, 128), jnp.int32),
            dma((4,)),
            dma((2, OWN_TILES, 2)),
            dma((2, 2, 11)),
            dma((2, 2, 11)),
            dma((2, 2, 2, OWN_TILES)),
            dma((2, 2, 2, OWN_TILES)),
            dma((2, 2, 2, OWN_TILES + 1)),
            dma((2, 2, 2, OWN_TILES + 1)),
            dma((SEQ,)),
            dma((SEQ,)),
        ],
        compiler_params=pltpu.CompilerParams(collective_id=0, has_side_effects=True),
        cost_estimate=pl.CostEstimate(
            flops=9_663_676_416, bytes_accessed=3_145_728, transcendentals=18_874_368
        ),
        name="attend",
    )(queries[0], keys[0], values[0], exit_layer, tile_order)
    return attended[None], live[0, :1]


def solution(mesh):
    parts = ("batch", "seq")
    return jax.shard_map(
        body,
        mesh=mesh,
        in_specs=(
            P(None, parts, "head"),
            P(None, parts, "head"),
            P(None, parts, "head"),
            P(parts),
            P("batch"),
        ),
        out_specs=(P(None, parts, "head"), P("batch")),
        check_vma=False,
    )
```

time: 321 us -> 94.9 us (0.30)
  the two profiles are of different devices: /device:TPU:1 before, /device:TPU:4 now
where the time goes in v1:
time: 94.9 us; the launch traced here: 94.7 us
  Pallas kernels  90.8 us (96%)
  local copies, waits for them, and re-layouts  3.25 us (3%)
    pallas_call x1, Pallas kernels, body(): pl.pallas_call(kernel, out_shape=(jax.ShapeDtypeStruct((ROWS, 4 * HD), bf...  90.8 us
    unnamed x1, local copies, waits for them, and re-layouts  2.06 us

profile of v1, /device:TPU:4, one launch (start us, length us, event | category | flops | bytes accessed | tf_op | source)
XLA Modules:
  0.0 94.7 jit_solution(16479073227999970418)
XLA Ops:
  0.6 90.8 %attend.1 = (bf16[384,1024]{1,0:T(8,128)(2,1)}, s32[8,128]{1,0:T(8,128)}) custom-call(bf16[384,1024]{1,0:T(8,128)(2,1)} %bitcast.6, bf16[384,512]{1,0:T(8,128)(2,1)} %bitcast.7, bf16[384,512]{1,0:T(8,128)(2,1)} %bitcast.8, s32[3]{0:T(128)} %exit_ref.1, s32[48]{0:T(128)} %order_ref.1), custom_call_target="tpu_custom_call" | custom-call | flops 9663676416 | bytes 3145728 | tf_op jit(solution)/shard_map/attend/pallas_call | solution.py:390
  91.4 1.2 %slice.3 = s32[1,1]{1,0:T(1,128)} slice(s32[8,128]{1,0:T(8,128)} %get-tuple-element.5), slice={[0:1], [0:1]} | slice | bytes 8 | tf_op jit(solution)/shard_map/slice | solution.py:428
  92.6 2.1 %copy.8 = bf16[1,384,1024]{2,1,0:T(8,128)(2,1)} copy(bf16[1,384,1024]{2,1,0:T(8,128)(2,1)} %bitcast.5) | data formatting | bytes 1572864

commit v2 on v0

v2 whole, which is shorter than its diff:
```python
import math

import jax
import jax.numpy as jnp
from jax import lax
from jax.experimental import pallas as pl
from jax.experimental.pallas import tpu as pltpu
from jax.sharding import PartitionSpec as P

MESH = pl.DeviceIdType.MESH
HD = 256
TILE = 128
ROWS = 384
TILES = 3
Z = 8
PAIRS = 12
SLOTS = 2 * PAIRS
SCORE_TO_TANH = 0.0625 / 50.0
TANH_TO_EXP2 = 50.0 * math.log2(math.e)

OWN_SLOT = (0, 1, 17)
FOUR_SLOT = (14, 16, 15)
FIRST_PAIR = {1: 1, 2: 4, 3: 9}
HELD_LAG = 2
END_LAG = 4
SEND_FIRST = (1, 2, 3)
SEND_AT = {1: (4,), 2: (5, 7), 3: (6, 8), 5: (9,), 6: (10,), 7: (11,)}


def slot_of(away, t, side):
    return 2 * (FIRST_PAIR[away] + t) + side


def slot_sources():
    found = {}
    for t in range(TILES):
        found[OWN_SLOT[t]] = (0, t)
        found[FOUR_SLOT[t]] = (4, t)
        for away in (1, 2, 3):
            found[slot_of(away, t, 0)] = (Z - away, t)
            found[slot_of(away, t, 1)] = (away, t)
    return found


def rows(t):
    return pl.ds(t * TILE, TILE)


def kernel(
    q_hbm, k_hbm, v_hbm, exit_ref, order_ref,
    out_hbm, live_ref,
    q_mine, kv_mine, q, kv, acc, den, y_held, four_held, o_send, exits, column, k_order, q_order,
    mine_in, q_mine_in, own_in, own_q_in, own_y_out, z_out, z_in, four_out, four_in, four_on, f_out, f_in,
    y_out, y_in, y_on, y_end, q_out, q_in, o_out, o_in, o_local, e_out, e_in, c_out, c_in,
):
    batch = lax.axis_index("batch")
    seq = lax.axis_index("seq")
    core = lax.axis_index("head")
    y_lo = lax.rem(batch, 2)
    y_hi = seq // Z
    z = lax.rem(seq, Z)
    hosted = lax.rem(z, 4)
    home = core == hosted // 2
    sibling = {"head": 1 - core}
    other_batch = batch + 1 - 2 * y_lo
    y_to = (
        {"batch": other_batch, "seq": lax.rem(y_hi + y_lo, 2) * Z + z},
        {"batch": other_batch, "seq": lax.rem(y_hi + 1 - y_lo, 2) * Z + z},
    )

    def chip(offset):
        return y_hi * Z + lax.rem(z + offset, Z)

    def remote(src, dst, sent, arrived, device):
        return pltpu.make_async_remote_copy(
            src_ref=src, dst_ref=dst, send_sem=sent, recv_sem=arrived,
            device_id=device, device_id_type=MESH,
        )

    def columns(n):
        return pl.ds(pl.multiple_of(n * HD, HD), HD)

    q_from = (0, Z - 1, 1, Z - 2 - 4 * core)

    own_column = lax.rem(hosted, 2)
    own_loads = [
        pltpu.make_async_copy(
            src.at[rows(t), columns(own_column)], kv.at[part, OWN_SLOT[t]], own_in.at[t, part]
        )
        for t in range(TILES)
        for part, src in ((0, k_hbm), (1, v_hbm))
    ]
    own_q_load = pltpu.make_async_copy(
        q_hbm.at[:, columns(2 * own_column + core)], q.at[0], own_q_in.at[0]
    )

    loads = [
        pltpu.make_async_copy(
            src.at[rows(t), pl.ds(j * HD, HD)], kv_mine.at[part, j, t], mine_in.at[part, j, t]
        )
        for t in range(TILES)
        for j in range(2)
        for part, src in ((0, k_hbm), (1, v_hbm))
    ] + [
        pltpu.make_async_copy(q_hbm.at[:, pl.ds(n * HD, HD)], q_mine.at[n], q_mine_in.at[n])
        for n in range(4)
    ]
    for load in loads:
        load.start()

    @pl.when(home)
    def _():
        for load in own_loads:
            load.start()
        own_q_load.start()

    sublane = lax.broadcasted_iota(jnp.int32, (8, 128), 0)
    mine = jnp.zeros((8, 128), jnp.int32)
    for t in range(TILES):
        mine = jnp.where(sublane == t, exit_ref[t], mine)
    exits[0] = mine

    barrier = pltpu.get_barrier_semaphore()
    near = (1, 2, 3, 5, 6, 7)
    for offset in near:
        for c in range(2):
            pl.semaphore_signal(
                barrier, inc=1, device_id={"seq": chip(offset), "head": c}, device_id_type=MESH
            )
    for peer in y_to:
        for c in range(2):
            pl.semaphore_signal(
                barrier, inc=1, device_id={**peer, "head": c}, device_id_type=MESH
            )
    pl.semaphore_signal(barrier, inc=1, device_id=sibling, device_id_type=MESH)
    for load in loads:
        load.wait()
    pl.semaphore_wait(barrier, 2 * len(near) + 5)

    def q_copy(n, offset, c, index):
        head = lax.rem(z + offset, 4)
        return remote(
            q_mine.at[2 * lax.rem(head, 2) + c],
            q.at[index],
            q_out.at[n],
            q_in.at[index],
            {"seq": chip(offset), "head": c},
        )

    q_sends = []
    for n, (offset, c, index) in enumerate(
        ((2, 0, 3), (6, 1, 3), (1, 0, 1), (1, 1, 1), (7, 0, 2), (7, 1, 2))
    ):
        q_sends.append((lax.rem(z + offset, 4) // 2 == core, q_copy(n, offset, c, index)))
    own_q_send = remote(
        q_mine.at[2 * own_column + 1 - core], q.at[0], q_out.at[6], q_in.at[0], sibling
    )
    own_y_sends = [
        remote(
            kv_mine.at[part, own_column, t], y_held.at[OWN_SLOT[t]],
            own_y_out.at[t, part], y_in.at[OWN_SLOT[t]],
            {**y_to[OWN_SLOT[t] % 2], "head": part},
        )
        for t in range(TILES)
        for part in range(2)
    ]

    @pl.when(home)
    def _():
        for copy in own_y_sends:
            copy.start()

    for holds, copy in q_sends:

        @pl.when(holds)
        def _():
            copy.start()

    pl.when(home)(own_q_send.start)

    def z_copies(away):
        found = []
        for t in range(TILES):
            for side in range(2):
                offset = away if side == 0 else Z - away
                head = lax.rem(z + offset, 4)
                for part in range(2):
                    slot = slot_of(away, t, side)
                    found.append((
                        head // 2 == core,
                        remote(
                            kv_mine.at[part, lax.rem(head, 2), t],
                            kv.at[part, slot],
                            z_out.at[part, slot],
                            z_in.at[slot],
                            {"seq": chip(offset), "head": part},
                        ),
                    ))
        return found

    def four_copies():
        found = []
        for n in range(2):
            for way in range(2):
                offset = 2 if way == 0 else Z - 2
                for part in range(2):
                    if n == 1 and part != way:
                        continue
                    t = 1 if n == 1 else 2 * way
                    found.append((
                        home,
                        remote(
                            kv_mine.at[part, own_column, t],
                            four_held.at[way, n],
                            four_out.at[way, n, part],
                            four_in.at[way, n],
                            {"seq": chip(offset), "head": part},
                        ),
                    ))
        return found

    by_pair = {}
    for away in (1, 2, 3):
        copies = z_copies(away)
        for t in range(TILES):
            by_pair[FIRST_PAIR[away] + t] = copies[4 * t : 4 * t + 4]
    four = four_copies()
    by_pair[7], by_pair[8] = four[:4], four[4:]
    kv_sends = [copy for copies in by_pair.values() for copy in copies]

    def start_all(copies):
        for holds, copy in copies:
            pl.when(holds)(copy.start)

    def f_copy(slot):
        return remote(
            kv.at[core, slot], kv.at[core, slot], f_out.at[slot], f_in.at[slot], sibling
        )

    def f_arrived(slot):
        return remote(
            kv.at[1 - core, slot], kv.at[1 - core, slot], f_out.at[slot], f_in.at[slot], sibling
        )

    def own_copy(t):
        slot = OWN_SLOT[t]
        return remote(
            kv.at[1 - core, slot], kv.at[1 - core, slot],
            z_out.at[0, slot], z_in.at[slot], sibling,
        )

    def z_arrived(slot):
        return remote(
            kv.at[core, slot], kv.at[core, slot], f_out.at[slot], z_in.at[slot], sibling
        )

    def y_first(slot, side):
        return remote(
            kv.at[core, slot], y_held.at[slot], y_out.at[slot], y_in.at[slot], y_to[side]
        )

    def y_second(slot, side):
        return remote(
            y_held.at[slot], kv.at[core, SLOTS + slot], y_on.at[slot], y_end.at[slot], y_to[side]
        )

    def four_forward(way, n):
        slot = FOUR_SLOT[1] if n == 1 else FOUR_SLOT[2 * way]
        return remote(
            four_held.at[way, n], kv.at[core, slot], four_on.at[way, n], z_in.at[slot],
            {"seq": chip(2 if way == 0 else Z - 2)},
        )

    for pair in SEND_FIRST:
        start_all(by_pair[pair])

    def exit_copy(offset):
        back = Z - offset
        return remote(
            exits.at[0], exits.at[back], e_out.at[offset], e_in.at[back], {"seq": chip(offset)}
        )

    exit_on = remote(exits.at[2], exits.at[4], e_out.at[4], e_in.at[4], {"seq": chip(Z - 2)})
    for offset in near:
        exit_copy(offset).start()

    @pl.when(home)
    def _():
        for load in own_loads:
            load.wait()
        for t in range(TILES):
            own_copy(t).start()
            f_copy(OWN_SLOT[t]).start()

    @pl.when(jnp.logical_not(home))
    def _():
        for t in range(TILES):
            z_arrived(OWN_SLOT[t]).wait_recv()

    acc[...] = jnp.zeros_like(acc)
    den[...] = jnp.zeros_like(den)
    for slot, (offset, t) in slot_sources().items():
        there = lax.rem(z + offset, Z)
        for other in range(2):
            k_order[other * SLOTS + slot] = order_ref[
                (lax.rem(y_hi + other, 2) * Z + there) * TILES + t
            ]
    for m, offset in enumerate(q_from):
        for t in range(TILES):
            q_order[m * TILES + t] = order_ref[chip(offset) * TILES + t]

    ahead = lax.broadcasted_iota(jnp.int32, (TILE, TILE), 1) - lax.broadcasted_iota(
        jnp.int32, (TILE, TILE), 0
    )

    def work(pair, half):
        query = q[pl.ds(2 * half, 2)].reshape(2 * ROWS, HD)
        key = kv[0, pl.ds(2 * pair, 2)].reshape(2 * TILE, HD)
        value = kv[1, pl.ds(2 * pair, 2)].reshape(2 * TILE, HD)
        score = lax.dot_general(
            query, key, (((1,), (1,)), ((), ())), preferred_element_type=jnp.float32
        )
        weight = jnp.exp2(jnp.tanh(score * SCORE_TO_TANH) * TANH_TO_EXP2)
        left_order = k_order[2 * pair]
        right_order = k_order[2 * pair + 1]
        blocks = []
        for m in range(2):
            for t in range(TILES):
                lower = (m * TILES + t) * TILE
                both = weight[lower : lower + TILE]
                mine = q_order[(2 * half + m) * TILES + t]
                left = jnp.where(ahead <= (mine - left_order) * TILE, both[:, :TILE], 0.0)
                right = jnp.where(ahead <= (mine - right_order) * TILE, both[:, TILE:], 0.0)
                den[2 * half + m, rows(t)] += left + right
                blocks.append(jnp.concatenate([left, right], axis=1).astype(jnp.bfloat16))
        product = jnp.dot(
            jnp.concatenate(blocks, axis=0), value, preferred_element_type=jnp.float32
        )
        acc[pl.ds(2 * half, 2)] += product.reshape(2, ROWS, HD)

    def both_parts(pair):
        for side in range(2):
            slot = 2 * pair + side
            owned = (slot == OWN_SLOT[0]) | (slot == OWN_SLOT[1]) | (slot == OWN_SLOT[2])

            @pl.when(jnp.logical_not(owned & home))
            def _():
                f_arrived(slot).wait_recv()

    def each_slot(p, act):
        for side in range(2):

            @pl.when(jnp.logical_not((p == 8) & (side == 1)))
            def _():
                act(2 * p + side, side)

        @pl.when(p == 0)
        def _():
            act(OWN_SLOT[2], 1)

    def arrive_z(slot, side):
        z_arrived(slot).wait_recv()
        f_copy(slot).start()
        y_first(slot, side).start()

    def arrive_held(slot, side):
        y_first(slot, side).wait_recv()
        y_second(slot, side).start()

    def arrive_y(slot, side):
        y_second(slot, side).wait_recv()
        f_copy(SLOTS + slot).start()

    def step(p, carry):
        @pl.when(p == 7)
        def _():
            for way in range(2):
                four_forward_in = remote(
                    four_held.at[way, 0], four_held.at[way, 0],
                    four_on.at[way, 0], four_in.at[way, 0], sibling,
                )
                four_forward_in.wait_recv()
                four_forward(way, 0).start()
            for way in range(2):

                @pl.when(core == way)
                def _():
                    remote(
                        four_held.at[way, 1], four_held.at[way, 1],
                        four_on.at[way, 1], four_in.at[way, 1], sibling,
                    ).wait_recv()
                    four_forward(way, 1).start()

        @pl.when(p >= END_LAG)
        def _():
            each_slot(p - END_LAG, arrive_y)

        @pl.when((p >= HELD_LAG) & (p < PAIRS + HELD_LAG))
        def _():
            each_slot(p - HELD_LAG, arrive_held)

        @pl.when((p >= 1) & (p <= PAIRS - 1))
        def _():
            each_slot(p, arrive_z)

        for at, pairs in SEND_AT.items():

            @pl.when(p == at)
            def _():
                for pair in pairs:
                    start_all(by_pair[pair])

        @pl.when(p == 1)
        def _():
            pl.when(home)(own_q_load.wait)
            for m in range(4):

                @pl.when(jnp.logical_not(home) if m == 0 else m > 0)
                def _():
                    remote(q.at[m], q.at[m], q_out.at[m], q_in.at[m], sibling).wait_recv()

        @pl.when((p >= 1) & (p <= PAIRS))
        def _():
            both_parts(p - 1)

        @pl.when(p > END_LAG)
        def _():
            both_parts(PAIRS + p - END_LAG - 1)

        first = jnp.where((p >= 1) & (p <= PAIRS), 0, 2)
        last = jnp.where(p > END_LAG, 4, 2)

        def item(n, c):
            work(jnp.where(n < 2, p - 1, PAIRS + p - END_LAG - 1), lax.rem(n, 2))
            return c

        lax.fori_loop(first, last, item, 0)

        @pl.when(p == 3)
        def _():
            remote(exits.at[2], exits.at[2], e_out.at[2], e_in.at[2], sibling).wait_recv()
            exit_on.start()

        @pl.when(p == 6)
        def _():
            for offset in (1, 3, 4, 5, 6, 7):
                remote(
                    exits.at[offset], exits.at[offset],
                    e_out.at[offset], e_in.at[offset], sibling,
                ).wait_recv()
            alive = jnp.zeros((8, 128), jnp.int32)
            for offset in range(Z):
                alive = alive + (exits[offset] > 0).astype(jnp.int32)
            column[0] = jnp.broadcast_to(jnp.sum(alive, axis=0, keepdims=True), (8, 128))

        pl.when(p == 7)(count_first.start)

        @pl.when(p == 9)
        def _():
            count_first.wait_recv()
            count_second.start()

        return carry

    count_first = remote(column.at[0], column.at[1], c_out.at[0], c_in.at[0], y_to[0])
    count_second = remote(column.at[1], column.at[2], c_out.at[1], c_in.at[1], y_to[0])

    lax.fori_loop(0, PAIRS + END_LAG, step, 0)

    def o_copy(m, t):
        return remote(
            o_send.at[m, rows(t)],
            out_hbm.at[rows(t), columns(2 * own_column + core)],
            o_out.at[m, t],
            o_in.at[2 * own_column + core, t],
            {"seq": chip(q_from[m]), "head": hosted // 2},
        )

    def o_here(t):
        return pltpu.make_async_copy(
            o_send.at[0, rows(t)],
            out_hbm.at[rows(t), columns(2 * own_column + core)],
            o_local.at[t],
        )

    def finish(m):
        for t in range(TILES):
            inverse = 1.0 / jnp.sum(den[m, rows(t)], axis=1, keepdims=True)
            alive = jnp.broadcast_to(exits[q_from[m], t : t + 1], (TILE, TILE)) > 0
            for lanes in (pl.ds(0, TILE), pl.ds(TILE, TILE)):
                o_send[m, rows(t), lanes] = jnp.where(
                    alive, acc[m, rows(t), lanes] * inverse, 0.0
                ).astype(jnp.bfloat16)
            if m == 0:
                pl.when(home)(o_here(t).start)
                pl.when(jnp.logical_not(home))(o_copy(m, t).start)
            else:
                o_copy(m, t).start()

    both_parts(2 * PAIRS - 1)
    work(2 * PAIRS - 1, 1)
    finish(3)
    finish(2)
    work(2 * PAIRS - 1, 0)
    finish(1)
    finish(0)

    count_second.wait_recv()
    live_ref[...] = column[0] + column[2]

    for holds, copy in q_sends + kv_sends:
        pl.when(holds)(copy.wait_send)
    for offset in near:
        exit_copy(offset).wait_send()
    exit_on.wait_send()
    count_first.wait_send()
    count_second.wait_send()
    for way in range(2):
        four_forward(way, 0).wait_send()
        pl.when(core == way)(four_forward(way, 1).wait_send)

    @pl.when(home)
    def _():
        own_q_send.wait_send()
        for copy in own_y_sends:
            copy.wait_send()
        for t in range(TILES):
            own_copy(t).wait_send()
            o_here(t).wait()

    @pl.when(jnp.logical_not(home))
    def _():
        for t in range(TILES):
            o_copy(0, t).wait_send()

    def sent(slot, carry):
        owned = (slot == OWN_SLOT[0]) | (slot == OWN_SLOT[1]) | (slot == OWN_SLOT[2])

        @pl.when(jnp.logical_not(owned) | home)
        def _():
            f_copy(slot).wait_send()

        f_copy(SLOTS + slot).wait_send()

        @pl.when(jnp.logical_not(owned))
        def _():
            y_first(slot, 0).wait_send()

        y_second(slot, 0).wait_send()
        return carry

    lax.fori_loop(0, SLOTS, sent, 0)
    for m in range(1, 4):
        for t in range(TILES):
            o_copy(m, t).wait_send()
    for n in range(4):
        local = home & (2 * own_column + core == n)
        for t in range(TILES):

            @pl.when(jnp.logical_not(local))
            def _():
                remote(
                    o_send.at[0, rows(t)],
                    out_hbm.at[rows(t), pl.ds(n * HD, HD)],
                    o_out.at[0, t], o_in.at[n, t], sibling,
                ).wait_recv()


def body(queries, keys, values, exit_layer, tile_order):
    hbm = pl.BlockSpec(memory_space=pltpu.HBM)
    smem = pl.BlockSpec(memory_space=pltpu.SMEM)
    vmem = pl.BlockSpec(memory_space=pltpu.VMEM)
    bf16, f32, i32 = jnp.bfloat16, jnp.float32, jnp.int32
    dma = pltpu.SemaphoreType.DMA
    attended, live = pl.pallas_call(
        kernel,
        out_shape=(
            jax.ShapeDtypeStruct((ROWS, 4 * HD), bf16),
            jax.ShapeDtypeStruct((8, 128), i32),
        ),
        in_specs=[hbm, hbm, hbm, smem, smem],
        out_specs=(hbm, vmem),
        scratch_shapes=[
            pltpu.VMEM((4, ROWS, HD), bf16),
            pltpu.VMEM((2, 2, TILES, TILE, HD), bf16),
            pltpu.VMEM((4, ROWS, HD), bf16),
            pltpu.VMEM((2, 2 * SLOTS, TILE, HD), bf16),
            pltpu.VMEM((4, ROWS, HD), f32),
            pltpu.VMEM((4, ROWS, TILE), f32),
            pltpu.VMEM((SLOTS, TILE, HD), bf16),
            pltpu.VMEM((2, 2, TILE, HD), bf16),
            pltpu.VMEM((4, ROWS, HD), bf16),
            pltpu.VMEM((Z, 8, 128), i32),
            pltpu.VMEM((3, 8, 128), i32),
            pltpu.SMEM((2 * SLOTS,), i32),
            pltpu.SMEM((4 * TILES,), i32),
            dma((2, 2, TILES)),
            dma((4,)),
            dma((TILES, 2)),
            dma((1,)),
            dma((TILES, 2)),
            dma((2, SLOTS)),
            dma((SLOTS,)),
            dma((2, 2, 2)),
            dma((2, 2)),
            dma((2, 2)),
            dma((2 * SLOTS,)),
            dma((2 * SLOTS,)),
            dma((SLOTS,)),
            dma((SLOTS,)),
            dma((SLOTS,)),
            dma((SLOTS,)),
            dma((7,)),
            dma((4,)),
            dma((4, TILES)),
            dma((4, TILES)),
            dma((TILES,)),
            dma((Z,)),
            dma((Z,)),
            dma((2,)),
            dma((2,)),
        ],
        compiler_params=pltpu.CompilerParams(collective_id=0, has_side_effects=True),
        cost_estimate=pl.CostEstimate(
            flops=9_663_676_416, bytes_accessed=3_145_728, transcendentals=18_874_368
        ),
        name="attend",
    )(queries[0], keys[0], values[0], exit_layer, tile_order)
    return attended[None], live[0, :1]


def solution(mesh):
    parts = ("batch", "seq")
    return jax.shard_map(
        body,
        mesh=mesh,
        in_specs=(
            P(None, parts, "head"),
            P(None, parts, "head"),
            P(None, parts, "head"),
            P(parts),
            P("batch"),
        ),
        out_specs=(P(None, parts, "head"), P("batch")),
        check_vma=False,
    )
```

time: 321 us -> 90.6 us (0.28)
  waiting for transfers between devices: 169 us -> 0 us
  matrix products: 90 us -> 0 us
  Pallas kernels: 0 us -> 86.6 us
  blocking collectives: 19.9 us -> 0 us
  between operations: 14.2 us -> 0.64 us
  local copies, waits for them, and re-layouts: 16.7 us -> 3.25 us
  other arithmetic: 7.52 us -> 0 us
    all_gather x1 -> x0, waiting for transfers between devices: 169 us -> none  [side_by_side(): lax.all_gather(both, axis, axis=dim, tiled=True)]
    dot_general x24 -> x0, matrix products: 90 us -> none  [the longest x12 47.3 us: one_block(): jnp.einsum('tkgd,skd->kgts', grouped, key_block, preferred_element_type=j...]
    pallas_call x0 -> x1, Pallas kernels: none -> 86.6 us  [body(): pl.pallas_call(kernel, out_shape=(jax.ShapeDtypeStruct((ROWS, 4 * HD), bf...]
    psum x2 -> x0, blocking collectives: 19.9 us -> none  [by_axis(): x = lax.psum(x, axis)]
    slice x1, local copies, waits for them, and re-layouts: 10.6 us -> 1.19 us  [body(): return (attended[None], live[0, :1])]
  transfers between devices with their start and end apart: 1 -> 0, of which waited for: 1 -> 0; matrix products, arithmetic and copies ran while one was open for 1% -> 0% of each run, Pallas kernels for 0% -> 0%
where the time goes in v2:
time: 90.6 us; the launch traced here: 90.4 us
  Pallas kernels  86.6 us (96%)
  local copies, waits for them, and re-layouts  3.25 us (4%)
    pallas_call x1, Pallas kernels, body(): pl.pallas_call(kernel, out_shape=(jax.ShapeDtypeStruct((ROWS, 4 * HD), bf...  86.6 us
    unnamed x1, local copies, waits for them, and re-layouts  2.06 us

profile of v2, /device:TPU:1, one launch (start us, length us, event | category | flops | bytes accessed | tf_op | source)
XLA Modules:
  0.0 90.4 jit_solution(15779178621177729405)
XLA Ops:
  0.6 86.6 %attend.1 = (bf16[384,1024]{1,0:T(8,128)(2,1)}, s32[8,128]{1,0:T(8,128)}) custom-call(bf16[384,1024]{1,0:T(8,128)(2,1)} %bitcast.6, bf16[384,512]{1,0:T(8,128)(2,1)} %bitcast.7, bf16[384,512]{1,0:T(8,128)(2,1)} %bitcast.8, s32[3]{0:T(128)} %exit_ref.1, s32[48]{0:T(128)} %order_ref.1), custom_call_target="tpu_custom_call" | custom-call | flops 9663676416 | bytes 3145728 | tf_op jit(solution)/shard_map/attend/pallas_call | solution.py:575
  87.2 1.2 %slice.3 = s32[1,1]{1,0:T(1,128)} slice(s32[8,128]{1,0:T(8,128)} %get-tuple-element.5), slice={[0:1], [0:1]} | slice | bytes 8 | tf_op jit(solution)/shard_map/slice | solution.py:629
  88.4 2.1 %copy.8 = bf16[1,384,1024]{2,1,0:T(8,128)(2,1)} copy(bf16[1,384,1024]{2,1,0:T(8,128)(2,1)} %bitcast.5) | data formatting | bytes 1572864

commit v3 on v2

--- a/solution.py
+++ b/solution.py
@@ -18,13 +18,14 @@
 SCORE_TO_TANH = 0.0625 / 50.0
 TANH_TO_EXP2 = 50.0 * math.log2(math.e)
 
-OWN_SLOT = (0, 1, 17)
-FOUR_SLOT = (14, 16, 15)
-FIRST_PAIR = {1: 1, 2: 4, 3: 9}
+OWN_SLOT = (0, 1, 23)
+FOUR_SLOT = (20, 22, 21)
+FIRST_PAIR = {1: 1, 2: 4, 3: 7}
 HELD_LAG = 2
 END_LAG = 4
-SEND_FIRST = (1, 2, 3)
-SEND_AT = {1: (4,), 2: (5, 7), 3: (6, 8), 5: (9,), 6: (10,), 7: (11,)}
+FOUR_STEP = 9
+SEND_FIRST = (1,2,3)
+SEND_AT = {1:(4,), 2:(5,), 3:(6,), 4:(7,), 5:(10,11), 6:(8,), 7:(9,)}
 
 
 def slot_of(away, t, side):
@@ -48,10 +49,10 @@
 
 def kernel(
     q_hbm, k_hbm, v_hbm, exit_ref, order_ref,
-    out_hbm, live_ref,
+    out, live_ref,
     q_mine, kv_mine, q, kv, acc, den, y_held, four_held, o_send, exits, column, k_order, q_order,
     mine_in, q_mine_in, own_in, own_q_in, own_y_out, z_out, z_in, four_out, four_in, four_on, f_out, f_in,
-    y_out, y_in, y_on, y_end, q_out, q_in, o_out, o_in, o_local, e_out, e_in, c_out, c_in,
+    y_out, y_in, y_on, y_end, q_out, q_in, o_out, o_in, e_out, e_in, c_out, c_in,
 ):
     batch = lax.axis_index("batch")
     seq = lax.axis_index("seq")
@@ -225,7 +226,7 @@
         for t in range(TILES):
             by_pair[FIRST_PAIR[away] + t] = copies[4 * t : 4 * t + 4]
     four = four_copies()
-    by_pair[7], by_pair[8] = four[:4], four[4:]
+    by_pair[10], by_pair[11] = four[:4], four[4:]
     kv_sends = [copy for copies in by_pair.values() for copy in copies]
 
     def start_all(copies):
@@ -313,30 +314,34 @@
         jnp.int32, (TILE, TILE), 0
     )
 
-    def work(pair, half):
-        query = q[pl.ds(2 * half, 2)].reshape(2 * ROWS, HD)
+    def work(pair, halves):
         key = kv[0, pl.ds(2 * pair, 2)].reshape(2 * TILE, HD)
         value = kv[1, pl.ds(2 * pair, 2)].reshape(2 * TILE, HD)
-        score = lax.dot_general(
-            query, key, (((1,), (1,)), ((), ())), preferred_element_type=jnp.float32
-        )
-        weight = jnp.exp2(jnp.tanh(score * SCORE_TO_TANH) * TANH_TO_EXP2)
         left_order = k_order[2 * pair]
         right_order = k_order[2 * pair + 1]
-        blocks = []
-        for m in range(2):
-            for t in range(TILES):
-                lower = (m * TILES + t) * TILE
-                both = weight[lower : lower + TILE]
-                mine = q_order[(2 * half + m) * TILES + t]
-                left = jnp.where(ahead <= (mine - left_order) * TILE, both[:, :TILE], 0.0)
-                right = jnp.where(ahead <= (mine - right_order) * TILE, both[:, TILE:], 0.0)
-                den[2 * half + m, rows(t)] += left + right
-                blocks.append(jnp.concatenate([left, right], axis=1).astype(jnp.bfloat16))
-        product = jnp.dot(
-            jnp.concatenate(blocks, axis=0), value, preferred_element_type=jnp.float32
-        )
-        acc[pl.ds(2 * half, 2)] += product.reshape(2, ROWS, HD)
+        scores = [
+            lax.dot_general(
+                q[pl.ds(2 * half, 2)].reshape(2 * ROWS, HD), key, (((1,), (1,)), ((), ())),
+                preferred_element_type=jnp.float32,
+            )
+            for half in halves
+        ]
+        for half, score in zip(halves, scores):
+            blocks = []
+            for m in range(2):
+                for t in range(TILES):
+                    lower = (m * TILES + t) * TILE
+                    both = score[lower : lower + TILE]
+                    both = jnp.exp2(jnp.tanh(both * SCORE_TO_TANH) * TANH_TO_EXP2)
+                    mine = q_order[(2 * half + m) * TILES + t]
+                    left = jnp.where(ahead <= (mine - left_order) * TILE, both[:, :TILE], 0.0)
+                    right = jnp.where(ahead <= (mine - right_order) * TILE, both[:, TILE:], 0.0)
+                    den[2 * half + m, rows(t)] += left + right
+                    blocks.append(jnp.concatenate([left, right], axis=1).astype(jnp.bfloat16))
+            product = jnp.dot(
+                jnp.concatenate(blocks, axis=0), value, preferred_element_type=jnp.float32
+            )
+            acc[pl.ds(2 * half, 2)] += product.reshape(2, ROWS, HD)
 
     def both_parts(pair):
         for side in range(2):
@@ -350,7 +355,7 @@
     def each_slot(p, act):
         for side in range(2):
 
-            @pl.when(jnp.logical_not((p == 8) & (side == 1)))
+            @pl.when(jnp.logical_not((p == PAIRS - 1) & (side == 1)))
             def _():
                 act(2 * p + side, side)
 
@@ -372,7 +377,7 @@
         f_copy(SLOTS + slot).start()
 
     def step(p, carry):
-        @pl.when(p == 7)
+        @pl.when(p == FOUR_STEP)
         def _():
             for way in range(2):
                 four_forward_in = remote(
@@ -427,11 +432,11 @@
         def _():
             both_parts(PAIRS + p - END_LAG - 1)
 
-        first = jnp.where((p >= 1) & (p <= PAIRS), 0, 2)
-        last = jnp.where(p > END_LAG, 4, 2)
+        first = jnp.where((p >= 1) & (p <= PAIRS), 0, 1)
+        last = jnp.where(p > END_LAG, 2, 1)
 
         def item(n, c):
-            work(jnp.where(n < 2, p - 1, PAIRS + p - END_LAG - 1), lax.rem(n, 2))
+            work(jnp.where(n < 1, p - 1, PAIRS + p - END_LAG - 1), (0, 1))
             return c
 
         lax.fori_loop(first, last, item, 0)
@@ -470,17 +475,10 @@
     def o_copy(m, t):
         return remote(
             o_send.at[m, rows(t)],
-            out_hbm.at[rows(t), columns(2 * own_column + core)],
+            out.at[rows(t), columns(2 * own_column + core)],
             o_out.at[m, t],
             o_in.at[2 * own_column + core, t],
             {"seq": chip(q_from[m]), "head": hosted // 2},
-        )
-
-    def o_here(t):
-        return pltpu.make_async_copy(
-            o_send.at[0, rows(t)],
-            out_hbm.at[rows(t), columns(2 * own_column + core)],
-            o_local.at[t],
         )
 
     def finish(m):
@@ -492,21 +490,25 @@
                     alive, acc[m, rows(t), lanes] * inverse, 0.0
                 ).astype(jnp.bfloat16)
             if m == 0:
-                pl.when(home)(o_here(t).start)
                 pl.when(jnp.logical_not(home))(o_copy(m, t).start)
+
+                @pl.when(home)
+                def _():
+                    out[rows(t), columns(2 * own_column + core)] = o_send[m, rows(t)]
+
             else:
                 o_copy(m, t).start()
 
     both_parts(2 * PAIRS - 1)
-    work(2 * PAIRS - 1, 1)
+    work(2 * PAIRS - 1, (1,))
     finish(3)
     finish(2)
-    work(2 * PAIRS - 1, 0)
+    work(2 * PAIRS - 1, (0,))
     finish(1)
     finish(0)
 
     count_second.wait_recv()
-    live_ref[...] = column[0] + column[2]
+    live_ref[0] = jnp.max(column[0] + column[2])
 
     for holds, copy in q_sends + kv_sends:
         pl.when(holds)(copy.wait_send)
@@ -526,7 +528,6 @@
             copy.wait_send()
         for t in range(TILES):
             own_copy(t).wait_send()
-            o_here(t).wait()
 
     @pl.when(jnp.logical_not(home))
     def _():
@@ -561,7 +562,7 @@
             def _():
                 remote(
                     o_send.at[0, rows(t)],
-                    out_hbm.at[rows(t), pl.ds(n * HD, HD)],
+                    out.at[rows(t), pl.ds(n * HD, HD)],
                     o_out.at[0, t], o_in.at[n, t], sibling,
                 ).wait_recv()
 
@@ -569,17 +570,16 @@
 def body(queries, keys, values, exit_layer, tile_order):
     hbm = pl.BlockSpec(memory_space=pltpu.HBM)
     smem = pl.BlockSpec(memory_space=pltpu.SMEM)
-    vmem = pl.BlockSpec(memory_space=pltpu.VMEM)
     bf16, f32, i32 = jnp.bfloat16, jnp.float32, jnp.int32
     dma = pltpu.SemaphoreType.DMA
     attended, live = pl.pallas_call(
         kernel,
         out_shape=(
-            jax.ShapeDtypeStruct((ROWS, 4 * HD), bf16),
-            jax.ShapeDtypeStruct((8, 128), i32),
+            pltpu.VMEM((ROWS, 4 * HD), bf16),
+            jax.ShapeDtypeStruct((1,), i32),
         ),
         in_specs=[hbm, hbm, hbm, smem, smem],
-        out_specs=(hbm, vmem),
+        out_specs=(pl.BlockSpec(memory_space=pltpu.VMEM), smem),
         scratch_shapes=[
             pltpu.VMEM((4, ROWS, HD), bf16),
             pltpu.VMEM((2, 2, TILES, TILE, HD), bf16),
@@ -614,7 +614,6 @@
             dma((4,)),
             dma((4, TILES)),
             dma((4, TILES)),
-            dma((TILES,)),
             dma((Z,)),
             dma((Z,)),
             dma((2,)),
@@ -626,7 +625,7 @@
         ),
         name="attend",
     )(queries[0], keys[0], values[0], exit_layer, tile_order)
-    return attended[None], live[0, :1]
+    return attended[None], live
 
 
 def solution(mesh):

time: 90.6 us -> 86.9 us (0.959)
  Pallas kernels: 86.6 us -> 83.6 us
  local copies, waits for them, and re-layouts: 3.25 us -> 0.88 us
  between operations: 0.64 us -> 2.33 us
    pallas_call x1, Pallas kernels: 86.6 us -> 83.6 us  [body(): pl.pallas_call(kernel, out_shape=(pltpu.VMEM((ROWS, 4 * HD), bf16), jax.S...]
    slice x1 -> x0, local copies, waits for them, and re-layouts: 1.19 us -> none  [body(): return (attended[None], live[0, :1])]
    unnamed x1, local copies, waits for them, and re-layouts: 2.06 us -> 0.88 us
where the time goes in v3:
time: 86.9 us; the launch traced here: 86.8 us
  Pallas kernels  83.6 us (96%)
  between operations  2.33 us (3%)
  local copies, waits for them, and re-layouts  0.88 us (1%)
    pallas_call x1, Pallas kernels, body(): pl.pallas_call(kernel, out_shape=(pltpu.VMEM((ROWS, 4 * HD), bf16), jax.S...  83.6 us

profile of v3, /device:TPU:1, one launch (start us, length us, event | category | flops | bytes accessed | tf_op | source)
XLA Modules:
  0.0 86.8 jit_solution(1390443215464304104)
XLA Ops:
  0.6 83.6 %attend.1 = (bf16[384,1024]{1,0:T(8,128)(2,1)S(1)}, s32[1]{0:T(128)}) custom-call(bf16[384,1024]{1,0:T(8,128)(2,1)} %bitcast.5, bf16[384,512]{1,0:T(8,128)(2,1)} %bitcast.6, bf16[384,512]{1,0:T(8,128)(2,1)} %bitcast.7, s32[3]{0:T(128)} %exit_ref.1, s32[48]{0:T(128)} %order_ref.1), custom_call_target="tpu_custom_call" | custom-call | flops 9663676416 | bytes 3145728 | tf_op jit(solution)/shard_map/attend/pallas_call | solution.py:575
  84.2 0.9 %copy.9 = bf16[1,384,1024]{2,1,0:T(8,128)(2,1)} copy(bf16[1,384,1024]{2,1,0:T(8,128)(2,1)S(1)} %bitcast.4) | data formatting | bytes 1572864

commit v4 on v3

--- a/solution.py
+++ b/solution.py
@@ -22,7 +22,7 @@
 FOUR_SLOT = (20, 22, 21)
 FIRST_PAIR = {1: 1, 2: 4, 3: 7}
 HELD_LAG = 2
-END_LAG = 4
+END_LAG = 5
 FOUR_STEP = 9
 SEND_FIRST = (1,2,3)
 SEND_AT = {1:(4,), 2:(5,), 3:(6,), 4:(7,), 5:(10,11), 6:(8,), 7:(9,)}
@@ -400,6 +400,11 @@
         def _():
             each_slot(p - END_LAG, arrive_y)
 
+        @pl.when(p > END_LAG)
+        def _():
+            both_parts(PAIRS + p - END_LAG - 1)
+            work(PAIRS + p - END_LAG - 1, (0, 1))
+
         @pl.when((p >= HELD_LAG) & (p < PAIRS + HELD_LAG))
         def _():
             each_slot(p - HELD_LAG, arrive_held)
@@ -427,19 +432,7 @@
         @pl.when((p >= 1) & (p <= PAIRS))
         def _():
             both_parts(p - 1)
-
-        @pl.when(p > END_LAG)
-        def _():
-            both_parts(PAIRS + p - END_LAG - 1)
-
-        first = jnp.where((p >= 1) & (p <= PAIRS), 0, 1)
-        last = jnp.where(p > END_LAG, 2, 1)
-
-        def item(n, c):
-            work(jnp.where(n < 1, p - 1, PAIRS + p - END_LAG - 1), (0, 1))
-            return c
-
-        lax.fori_loop(first, last, item, 0)
+            work(p - 1, (0, 1))
 
         @pl.when(p == 3)
         def _():

time: 86.9 us -> 84.7 us (0.975)
  Pallas kernels: 83.6 us -> 81.3 us
    pallas_call x1, Pallas kernels: 83.6 us -> 81.3 us  [body(): pl.pallas_call(kernel, out_shape=(pltpu.VMEM((ROWS, 4 * HD), bf16), jax.S...]
where the time goes in v4:
time: 84.7 us; the launch traced here: 84.5 us
  Pallas kernels  81.3 us (96%)
  between operations  2.33 us (3%)
  local copies, waits for them, and re-layouts  0.88 us (1%)
    pallas_call x1, Pallas kernels, body(): pl.pallas_call(kernel, out_shape=(pltpu.VMEM((ROWS, 4 * HD), bf16), jax.S...  81.3 us

profile of v4, /device:TPU:1, one launch (start us, length us, event | category | flops | bytes accessed | tf_op | source)
XLA Modules:
  0.0 84.5 jit_solution(5365013397578736696)
XLA Ops:
  0.6 81.3 %attend.1 = (bf16[384,1024]{1,0:T(8,128)(2,1)S(1)}, s32[1]{0:T(128)}) custom-call(bf16[384,1024]{1,0:T(8,128)(2,1)} %bitcast.5, bf16[384,512]{1,0:T(8,128)(2,1)} %bitcast.6, bf16[384,512]{1,0:T(8,128)(2,1)} %bitcast.7, s32[3]{0:T(128)} %exit_ref.1, s32[48]{0:T(128)} %order_ref.1), custom_call_target="tpu_custom_call" | custom-call | flops 9663676416 | bytes 3145728 | tf_op jit(solution)/shard_map/attend/pallas_call | solution.py:568
  82.0 0.9 %copy.9 = bf16[1,384,1024]{2,1,0:T(8,128)(2,1)} copy(bf16[1,384,1024]{2,1,0:T(8,128)(2,1)S(1)} %bitcast.4) | data formatting | bytes 1572864
